TPU v7x, 32 devices: a whole 2x2x4 slice. The times are simulated.
32 devices in a mesh: dp: 16 (over z, x, core), tensor: 2 (over y).
Axes of the slice: x: 2, y: 2, z: 4, core: 2. Of those that a mesh axis runs over, the one named last changes fastest.
Arguments:
- grad_hidden: bfloat16 [2048, 14336], P('dp', 'tensor'), may hold values from -18 to 18
- gate: bfloat16 [2048, 14336], P('dp', 'tensor'), may hold values from -6 to 6
Outputs:
- factor: float32 [14336, 14336], P('tensor', 'dp')
All inputs are finite; a program needn't handle non-finite values.
Results may differ from a plain program's by a relative error of at most 0.0065.
Values may be sent and summed in bfloat16 or wider, within the bound.
No kernel may reach another device: no remote copies, remote signals or barrier semaphores. Data moves between devices by JAX's collectives and lax.ppermute only.
A program may use at most 128 MiB of HBM per device.

v0:
```python
import jax
import jax.numpy as jnp
from jax import lax
from jax.sharding import PartitionSpec as P

FF = 14336


def shards(grad_hidden, gate):
    up_grad = (grad_hidden.astype(jnp.float32) * jax.nn.silu(gate.astype(jnp.float32))).astype(
        jnp.bfloat16
    )
    tensor_count = lax.axis_size("tensor")
    data_count = lax.axis_size("dp")
    col_width = FF // data_count
    ratio = data_count // tensor_count
    data_index = lax.axis_index("dp")
    owner = data_index // ratio
    offset = data_index % ratio * col_width
    contract = (((0,), (0,)), ((), ()))
    total_tokens = up_grad.shape[0] * data_count
    rows_all = lax.all_gather(up_grad, "dp", axis=0, tiled=True)
    panel = lax.dynamic_slice_in_dim(rows_all, offset, col_width, 1)
    slices = lax.all_gather(panel, "tensor", axis=1, tiled=True)
    cols_all = lax.dynamic_slice_in_dim(slices, owner * col_width, col_width, 1)
    summed = lax.dot_general(rows_all, cols_all, contract, preferred_element_type=jnp.float32)
    return summed / total_tokens


def solution(mesh):
    return jax.shard_map(
        shards,
        mesh=mesh,
        in_specs=(P("dp", "tensor"), P("dp", "tensor")),
        out_specs=P("tensor", "dp"),
        check_vma=False,
    )
```

profile of v0, /device:TPU:0, one launch (start us, length us, event | category | flops | bytes accessed | tf_op | source)
XLA Modules:
  0.0 303.7 jit_solution(14807854129925651823)
XLA Ops:
  6.5 0.0 all-gather.3.cloned.1.call-start
  6.5 4.4 %fusion.5 = bf16[128,7168]{1,0:T(8,128)(2,1)} fusion(bf16[128,7168]{1,0:T(8,128)(2,1)} %param.3, bf16[128,7168]{1,0:T(8,128)(2,1)} %param.2), kind=kLoop, calls=%fused_computation.8 | loop fusion | flops 7340032 | bytes 5505024 | tf_op jit(solution)/shard_map/convert_element_type | solution.py:10
  10.9 0.0 all-gather.3.cloned.1.call-update
  11.0 0.0 all-gather.5.cloned.1.call-start
  11.0 151.1 %all-gather.3.cloned.1.call-done = bf16[2048,7168]{1,0:T(8,128)(2,1)} async-done(((bf16[128,7168]{1,0:T(8,128)(2,1)}), bf16[2048,7168]{1,0:T(8,128)(2,1)}) %all-gather.3.cloned.1.call-update) | async-done | bytes 29360144 | tf_op jit(solution)/shard_map/all_gather | solution.py:22
  162.1 4.2 %constant_dynamic-slice_fusion = bf16[2048,896]{1,0:T(8,128)(2,1)} fusion(bf16[2048,7168]{1,0:T(8,128)(2,1)} %all-gather.3.cloned.1.call-done, s32[]{:T(128)S(6)} %select_n.18), kind=kLoop, calls=%fused_computation.10 | loop fusion | bytes 7340036 | tf_op jit(solution)/shard_map/dynamic_slice | solution.py:23
  166.3 0.0 all-gather.5.cloned.1.call-update
  166.3 92.3 %all-gather.5.cloned.1.call-done = bf16[2048,1792]{1,0:T(8,128)(2,1)} async-done(((bf16[2048,896]{1,0:T(8,128)(2,1)}), bf16[2048,1792]{1,0:T(8,128)(2,1)}) %all-gather.5.cloned.1.call-update) | async-done | bytes 7340048 | tf_op jit(solution)/shard_map/all_gather | solution.py:24
  258.6 38.3 %convolution_multiply_fusion = f32[7168,896]{1,0:T(8,128)} fusion(bf16[2048,7168]{1,0:T(8,128)(2,1)} %all-gather.3.cloned.1.call-done, bf16[2048,1792]{1,0:T(8,128)(2,1)} %all-gather.5.cloned.1.call-done, s32[]{:T(128)S(6)} %select_n.20), kind=kOutput, calls=%fused_computation | convolution fusion | flops 26313097216 | bytes 58720260 | tf_op jit(solution)/shard_map/dot_general | solution.py:26
Async XLA Ops:
  6.5 155.6 %all-gather.3.cloned.1.call-start = ((), (), s32[]{:S(2)}) async-start(), calls=%async_computation | async-start | bytes 31195136 | tf_op jit(solution)/shard_map/all_gather | solution.py:22
  11.0 247.7 %all-gather.5.cloned.1.call-start = ((), (), s32[]{:S(2)}) async-start(), calls=%async_computation.1 | async-start | bytes 11010048 | tf_op jit(solution)/shard_map/all_gather | solution.py:24
Sparse Core Ops, SparseCore 0:
  11.1 150.9 all-gather.2
  166.4 92.1 all-gather.4
where the time goes:
time: 304 us
  waiting for transfers between devices  243 us (80%)
  matrix products  38.3 us (13%)
  between operations  13.4 us (4%)
  other arithmetic  4.39 us (1%)
  local copies, waits for them, and re-layouts  4.17 us (1%)
    all_gather x1, waiting for transfers between devices, shards(): rows_all = lax.all_gather(up_grad, 'dp', axis=0, tiled=True)  151 us
    all_gather x1, waiting for transfers between devices, shards(): slices = lax.all_gather(panel, 'tensor', axis=1, tiled=True)  92.3 us
    dot_general x1, matrix products, shards(): lax.dot_general(rows_all, cols_all, contract, preferred_element_type=jnp....  38.3 us
  transfers between devices with their start and end apart: 2, of which 2 were waited for; matrix products, arithmetic and copies ran while one was open for 0% of the time, Pallas kernels for 0%

commit v1 on v0

--- a/solution.py
+++ b/solution.py
@@ -19,7 +19,12 @@
     offset = data_index % ratio * col_width
     contract = (((0,), (0,)), ((), ()))
     total_tokens = up_grad.shape[0] * data_count
-    rows_all = lax.all_gather(up_grad, "dp", axis=0, tiled=True)
+    ring = [up_grad]
+    for hop in range(15):
+        ring.append(lax.ppermute(ring[-1], "dp", [(dev, (dev + 1) % 16) for dev in range(16)]))
+    rows_all = jnp.roll(
+        jnp.concatenate(ring[::-1], axis=0), (lax.axis_index("dp") + 1) * ring[0].shape[0], axis=0
+    )
     panel = lax.dynamic_slice_in_dim(rows_all, offset, col_width, 1)
     slices = lax.all_gather(panel, "tensor", axis=1, tiled=True)
     cols_all = lax.dynamic_slice_in_dim(slices, owner * col_width, col_width, 1)

time: 304 us -> 620 us (2.04)
  waiting for transfers between devices: 243 us -> 471 us
  local copies, waits for them, and re-layouts: 4.17 us -> 92.1 us
    ppermute x0 -> x15, waiting for transfers between devices: none -> 381 us  [shards(): lax.ppermute(ring[-1], 'dp', [(dev, (dev + 1) % 16) for dev in range(16)])]
    all_gather x1 -> x0, waiting for transfers between devices: 151 us -> none  [shards(): rows_all = lax.all_gather(up_grad, 'dp', axis=0, tiled=True)]
    unnamed x0 -> x83, local copies, waits for them, and re-layouts: none -> 84.5 us
  transfers between devices with their start and end apart: 2 -> 16, of which waited for: 2 -> 16; matrix products, arithmetic and copies ran while one was open for 0% -> 0% of each run, Pallas kernels for 0% -> 0%
where the time goes in v1:
time: 620 us; the launch traced here: 619 us
  waiting for transfers between devices  471 us (76%)
  local copies, waits for them, and re-layouts  92.1 us (15%)
  matrix products  38.4 us (6%)
  between operations  13.6 us (2%)
    ppermute x15, waiting for transfers between devices, shards(): lax.ppermute(ring[-1], 'dp', [(dev, (dev + 1) % 16) for dev in range(16)])  381 us
    all_gather x1, waiting for transfers between devices, shards(): slices = lax.all_gather(panel, 'tensor', axis=1, tiled=True)  90.1 us
    unnamed x83, local copies, waits for them, and re-layouts  84.5 us
    dot_general x1, matrix products, shards(): lax.dot_general(rows_all, cols_all, contract, preferred_element_type=jnp....  38.4 us
  transfers between devices with their start and end apart: 16, of which 16 were waited for; matrix products, arithmetic and copies ran while one was open for 0% of the time, Pallas kernels for 0%

profile of v1, /device:TPU:0, one launch (start us, length us, event | category | flops | bytes accessed | tf_op | source)
XLA Modules:
  0.0 618.9 jit_solution(17043810119950618780)
XLA Ops:
  6.5 3.2 fusion.10
  10.2 25.9 %collective-permute-done = bf16[128,7168]{1,0:T(8,128)(2,1)S(1)} collective-permute-done((bf16[128,7168]{1,0:T(8,128)(2,1)S(1)}, bf16[128,7168]{1,0:T(8,128)(2,1)S(1)}, u32[]{:S(2)}, u32[]{:S(2)}) %collective-permute-start) | collective-permute-done | bytes 1835040 | tf_op jit(solution)/shard_map/ppermute | solution.py:24
  37.4 25.3 %collective-permute-done.1 = bf16[128,7168]{1,0:T(8,128)(2,1)S(1)} collective-permute-done((bf16[128,7168]{1,0:T(8,128)(2,1)S(1)}, bf16[128,7168]{1,0:T(8,128)(2,1)S(1)}, u32[]{:S(2)}, u32[]{:S(2)}) %collective-permute-start.1) | collective-permute-done | bytes 1835040 | tf_op jit(solution)/shard_map/ppermute | solution.py:24
  64.0 25.3 %collective-permute-done.2 = bf16[128,7168]{1,0:T(8,128)(2,1)S(1)} collective-permute-done((bf16[128,7168]{1,0:T(8,128)(2,1)S(1)}, bf16[128,7168]{1,0:T(8,128)(2,1)S(1)}, u32[]{:S(2)}, u32[]{:S(2)}) %collective-permute-start.2) | collective-permute-done | bytes 1835040 | tf_op jit(solution)/shard_map/ppermute | solution.py:24
  90.6 25.3 %collective-permute-done.3 = bf16[128,7168]{1,0:T(8,128)(2,1)S(1)} collective-permute-done((bf16[128,7168]{1,0:T(8,128)(2,1)S(1)}, bf16[128,7168]{1,0:T(8,128)(2,1)S(1)}, u32[]{:S(2)}, u32[]{:S(2)}) %collective-permute-start.3) | collective-permute-done | bytes 1835040 | tf_op jit(solution)/shard_map/ppermute | solution.py:24
  117.2 25.3 %collective-permute-done.4 = bf16[128,7168]{1,0:T(8,128)(2,1)S(1)} collective-permute-done((bf16[128,7168]{1,0:T(8,128)(2,1)S(1)}, bf16[128,7168]{1,0:T(8,128)(2,1)S(1)}, u32[]{:S(2)}, u32[]{:S(2)}) %collective-permute-start.4) | collective-permute-done | bytes 1835040 | tf_op jit(solution)/shard_map/ppermute | solution.py:24
  143.8 25.3 %collective-permute-done.5 = bf16[128,7168]{1,0:T(8,128)(2,1)S(1)} collective-permute-done((bf16[128,7168]{1,0:T(8,128)(2,1)S(1)}, bf16[128,7168]{1,0:T(8,128)(2,1)S(1)}, u32[]{:S(2)}, u32[]{:S(2)}) %collective-permute-start.5) | collective-permute-done | bytes 1835040 | tf_op jit(solution)/shard_map/ppermute | solution.py:24
  170.4 25.3 %collective-permute-done.6 = bf16[128,7168]{1,0:T(8,128)(2,1)S(1)} collective-permute-done((bf16[128,7168]{1,0:T(8,128)(2,1)S(1)}, bf16[128,7168]{1,0:T(8,128)(2,1)S(1)}, u32[]{:S(2)}, u32[]{:S(2)}) %collective-permute-start.6) | collective-permute-done | bytes 1835040 | tf_op jit(solution)/shard_map/ppermute | solution.py:24
  197.0 25.3 %collective-permute-done.7 = bf16[128,7168]{1,0:T(8,128)(2,1)S(1)} collective-permute-done((bf16[128,7168]{1,0:T(8,128)(2,1)S(1)}, bf16[128,7168]{1,0:T(8,128)(2,1)S(1)}, u32[]{:S(2)}, u32[]{:S(2)}) %collective-permute-start.7) | collective-permute-done | bytes 1835040 | tf_op jit(solution)/shard_map/ppermute | solution.py:24
  223.6 25.3 %collective-permute-done.8 = bf16[128,7168]{1,0:T(8,128)(2,1)S(1)} collective-permute-done((bf16[128,7168]{1,0:T(8,128)(2,1)S(1)}, bf16[128,7168]{1,0:T(8,128)(2,1)S(1)}, u32[]{:S(2)}, u32[]{:S(2)}) %collective-permute-start.8) | collective-permute-done | bytes 1835040 | tf_op jit(solution)/shard_map/ppermute | solution.py:24
  250.3 25.3 %collective-permute-done.9 = bf16[128,7168]{1,0:T(8,128)(2,1)S(1)} collective-permute-done((bf16[128,7168]{1,0:T(8,128)(2,1)S(1)}, bf16[128,7168]{1,0:T(8,128)(2,1)S(1)}, u32[]{:S(2)}, u32[]{:S(2)}) %collective-permute-start.9) | collective-permute-done | bytes 1835040 | tf_op jit(solution)/shard_map/ppermute | solution.py:24
  276.8 25.3 %collective-permute-done.10 = bf16[128,7168]{1,0:T(8,128)(2,1)S(1)} collective-permute-done((bf16[128,7168]{1,0:T(8,128)(2,1)S(1)}, bf16[128,7168]{1,0:T(8,128)(2,1)S(1)}, u32[]{:S(2)}, u32[]{:S(2)}) %collective-permute-start.10) | collective-permute-done | bytes 1835040 | tf_op jit(solution)/shard_map/ppermute | solution.py:24
  303.4 25.3 %collective-permute-done.11 = bf16[128,7168]{1,0:T(8,128)(2,1)S(1)} collective-permute-done((bf16[128,7168]{1,0:T(8,128)(2,1)S(1)}, bf16[128,7168]{1,0:T(8,128)(2,1)S(1)}, u32[]{:S(2)}, u32[]{:S(2)}) %collective-permute-start.11) | collective-permute-done | bytes 1835040 | tf_op jit(solution)/shard_map/ppermute | solution.py:24
  330.1 25.3 %collective-permute-done.12 = bf16[128,7168]{1,0:T(8,128)(2,1)S(1)} collective-permute-done((bf16[128,7168]{1,0:T(8,128)(2,1)S(1)}, bf16[128,7168]{1,0:T(8,128)(2,1)S(1)}, u32[]{:S(2)}, u32[]{:S(2)}) %collective-permute-start.12) | collective-permute-done | bytes 1835040 | tf_op jit(solution)/shard_map/ppermute | solution.py:24
  356.7 25.4 %collective-permute-done.13 = bf16[128,7168]{1,0:T(8,128)(2,1)} collective-permute-done((bf16[128,7168]{1,0:T(8,128)(2,1)S(1)}, bf16[128,7168]{1,0:T(8,128)(2,1)}, u32[]{:S(2)}, u32[]{:S(2)}) %collective-permute-start.13) | collective-permute-done | bytes 1835040 | tf_op jit(solution)/shard_map/ppermute | solution.py:24
  382.2 25.6 %collective-permute-done.14 = bf16[128,7168]{1,0:T(8,128)(2,1)} collective-permute-done((bf16[128,7168]{1,0:T(8,128)(2,1)}, bf16[128,7168]{1,0:T(8,128)(2,1)}, u32[]{:S(2)}, u32[]{:S(2)}) %collective-permute-start.14) | collective-permute-done | bytes 1835040 | tf_op jit(solution)/shard_map/ppermute | solution.py:24
  407.8 2.9 constant_dynamic-update-slice_fusion.31
  410.6 2.9 constant_dynamic-update-slice_fusion.30
  413.5 2.9 constant_dynamic-update-slice_fusion.29
  416.4 2.9 constant_dynamic-update-slice_fusion.28
  419.2 3.0 constant_dynamic-update-slice_fusion.27
  425.0 2.9 constant_dynamic-update-slice_fusion.25
  428.0 2.8 constant_dynamic-update-slice_fusion.24
  430.8 2.9 constant_dynamic-update-slice_fusion.23
  433.7 2.9 constant_dynamic-update-slice_fusion.22
  439.4 2.9 constant_dynamic-update-slice_fusion.20
  442.2 2.9 constant_dynamic-update-slice_fusion.19
  445.1 2.9 constant_dynamic-update-slice_fusion.18
  448.0 2.8 constant_dynamic-update-slice_fusion.17
  477.3 6.2 %dynamic_slice.11 = bf16[2048,896]{1,0:T(8,128)(2,1)} dynamic-slice(bf16[4096,7168]{1,0:T(8,128)(2,1)} %constant_dynamic-update-slice_fusion, s32[]{:T(128)S(6)} %select_n.35, s32[]{:T(128)S(6)} %select_n.38), dynamic_slice_sizes={2048,896} | dynamic-slice | bytes 7340036 | tf_op jit(solution)/shard_map/dynamic_slice | solution.py:28
  483.6 90.1 %all-gather.2.cloned.1.call-done = bf16[2048,1792]{1,0:T(8,128)(2,1)} async-done(((bf16[2048,896]{1,0:T(8,128)(2,1)}), bf16[2048,1792]{1,0:T(8,128)(2,1)}) %all-gather.2.cloned.1.call-update) | async-done | bytes 7340048 | tf_op jit(solution)/shard_map/all_gather | solution.py:29
  573.6 38.4 %fusion.2 = f32[7168,896]{1,0:T(8,128)} fusion(bf16[4096,7168]{1,0:T(8,128)(2,1)} %constant_dynamic-update-slice_fusion, s32[]{:T(128)S(6)} %select_n.34, bf16[2048,1792]{1,0:T(8,128)(2,1)} %all-gather.2.cloned.1.call-done, s32[]{:T(128)S(6)} %select_n.40), kind=kOutput, calls=%fused_computation.2 | convolution fusion | flops 26313097216 | bytes 58720264 | tf_op jit(solution)/shard_map/dot_general | solution.py:31
  (88 shorter events, 49.1 us)
Async XLA Ops:
  6.5 567.1 %all-gather.2.cloned.1.call-start = ((), (), s32[]{:S(2)}) async-start(), calls=%async_computation | async-start | bytes 11010048 | tf_op jit(solution)/shard_map/all_gather | solution.py:29
  9.7 26.4 %collective-permute-start = (bf16[128,7168]{1,0:T(8,128)(2,1)S(1)}, bf16[128,7168]{1,0:T(8,128)(2,1)S(1)}, u32[]{:S(2)}, u32[]{:S(2)}) collective-permute-start(bf16[128,7168]{1,0:T(8,128)(2,1)S(1)} %fusion.10), channel_id=1, source_target_pairs={{0,2},{2,4},{4,6},{6,8},{8,10},{10,12},{12,14},{14,16},{16,18},{18... | collective-permute-start | bytes 5505032 | tf_op jit(solution)/shard_map/ppermute | solution.py:24
  37.4 25.3 %collective-permute-start.1 = (bf16[128,7168]{1,0:T(8,128)(2,1)S(1)}, bf16[128,7168]{1,0:T(8,128)(2,1)S(1)}, u32[]{:S(2)}, u32[]{:S(2)}) collective-permute-start(bf16[128,7168]{1,0:T(8,128)(2,1)S(1)} %collective-permute-done), channel_id=1, source_target_pairs={{0,2},{2,4},{4,6},{6,8},{8,10},{10,12},{12,14},{14,16},{16,18},{18... | collective-permute-start | bytes 5505032 | tf_op jit(solution)/shard_map/ppermute | solution.py:24
  64.0 25.3 %collective-permute-start.2 = (bf16[128,7168]{1,0:T(8,128)(2,1)S(1)}, bf16[128,7168]{1,0:T(8,128)(2,1)S(1)}, u32[]{:S(2)}, u32[]{:S(2)}) collective-permute-start(bf16[128,7168]{1,0:T(8,128)(2,1)S(1)} %collective-permute-done.1), channel_id=1, source_target_pairs={{0,2},{2,4},{4,6},{6,8},{8,10},{10,12},{12,14},{14,16},{16,18},{18... | collective-permute-start | bytes 5505032 | tf_op jit(solution)/shard_map/ppermute | solution.py:24
  90.6 25.3 %collective-permute-start.3 = (bf16[128,7168]{1,0:T(8,128)(2,1)S(1)}, bf16[128,7168]{1,0:T(8,128)(2,1)S(1)}, u32[]{:S(2)}, u32[]{:S(2)}) collective-permute-start(bf16[128,7168]{1,0:T(8,128)(2,1)S(1)} %collective-permute-done.2), channel_id=1, source_target_pairs={{0,2},{2,4},{4,6},{6,8},{8,10},{10,12},{12,14},{14,16},{16,18},{18... | collective-permute-start | bytes 5505032 | tf_op jit(solution)/shard_map/ppermute | solution.py:24
  117.2 25.3 %collective-permute-start.4 = (bf16[128,7168]{1,0:T(8,128)(2,1)S(1)}, bf16[128,7168]{1,0:T(8,128)(2,1)S(1)}, u32[]{:S(2)}, u32[]{:S(2)}) collective-permute-start(bf16[128,7168]{1,0:T(8,128)(2,1)S(1)} %collective-permute-done.3), channel_id=1, source_target_pairs={{0,2},{2,4},{4,6},{6,8},{8,10},{10,12},{12,14},{14,16},{16,18},{18... | collective-permute-start | bytes 5505032 | tf_op jit(solution)/shard_map/ppermute | solution.py:24
  143.8 25.3 %collective-permute-start.5 = (bf16[128,7168]{1,0:T(8,128)(2,1)S(1)}, bf16[128,7168]{1,0:T(8,128)(2,1)S(1)}, u32[]{:S(2)}, u32[]{:S(2)}) collective-permute-start(bf16[128,7168]{1,0:T(8,128)(2,1)S(1)} %collective-permute-done.4), channel_id=1, source_target_pairs={{0,2},{2,4},{4,6},{6,8},{8,10},{10,12},{12,14},{14,16},{16,18},{18... | collective-permute-start | bytes 5505032 | tf_op jit(solution)/shard_map/ppermute | solution.py:24
  170.4 25.3 %collective-permute-start.6 = (bf16[128,7168]{1,0:T(8,128)(2,1)S(1)}, bf16[128,7168]{1,0:T(8,128)(2,1)S(1)}, u32[]{:S(2)}, u32[]{:S(2)}) collective-permute-start(bf16[128,7168]{1,0:T(8,128)(2,1)S(1)} %collective-permute-done.5), channel_id=1, source_target_pairs={{0,2},{2,4},{4,6},{6,8},{8,10},{10,12},{12,14},{14,16},{16,18},{18... | collective-permute-start | bytes 5505032 | tf_op jit(solution)/shard_map/ppermute | solution.py:24
  195.7 1.3 copy-start.12
  197.0 25.3 %collective-permute-start.7 = (bf16[128,7168]{1,0:T(8,128)(2,1)S(1)}, bf16[128,7168]{1,0:T(8,128)(2,1)S(1)}, u32[]{:S(2)}, u32[]{:S(2)}) collective-permute-start(bf16[128,7168]{1,0:T(8,128)(2,1)S(1)} %collective-permute-done.6), channel_id=1, source_target_pairs={{0,2},{2,4},{4,6},{6,8},{8,10},{10,12},{12,14},{14,16},{16,18},{18... | collective-permute-start | bytes 5505032 | tf_op jit(solution)/shard_map/ppermute | solution.py:24
  223.6 25.3 %collective-permute-start.8 = (bf16[128,7168]{1,0:T(8,128)(2,1)S(1)}, bf16[128,7168]{1,0:T(8,128)(2,1)S(1)}, u32[]{:S(2)}, u32[]{:S(2)}) collective-permute-start(bf16[128,7168]{1,0:T(8,128)(2,1)S(1)} %collective-permute-done.7), channel_id=1, source_target_pairs={{0,2},{2,4},{4,6},{6,8},{8,10},{10,12},{12,14},{14,16},{16,18},{18... | collective-permute-start | bytes 5505032 | tf_op jit(solution)/shard_map/ppermute | solution.py:24
  249.0 1.3 copy-start.16
  250.3 25.3 %collective-permute-start.9 = (bf16[128,7168]{1,0:T(8,128)(2,1)S(1)}, bf16[128,7168]{1,0:T(8,128)(2,1)S(1)}, u32[]{:S(2)}, u32[]{:S(2)}) collective-permute-start(bf16[128,7168]{1,0:T(8,128)(2,1)S(1)} %collective-permute-done.8), channel_id=1, source_target_pairs={{0,2},{2,4},{4,6},{6,8},{8,10},{10,12},{12,14},{14,16},{16,18},{18... | collective-permute-start | bytes 5505032 | tf_op jit(solution)/shard_map/ppermute | solution.py:24
  276.8 25.3 %collective-permute-start.10 = (bf16[128,7168]{1,0:T(8,128)(2,1)S(1)}, bf16[128,7168]{1,0:T(8,128)(2,1)S(1)}, u32[]{:S(2)}, u32[]{:S(2)}) collective-permute-start(bf16[128,7168]{1,0:T(8,128)(2,1)S(1)} %collective-permute-done.9), channel_id=1, source_target_pairs={{0,2},{2,4},{4,6},{6,8},{8,10},{10,12},{12,14},{14,16},{16,18},{18... | collective-permute-start | bytes 5505032 | tf_op jit(solution)/shard_map/ppermute | solution.py:24
  303.4 25.3 %collective-permute-start.11 = (bf16[128,7168]{1,0:T(8,128)(2,1)S(1)}, bf16[128,7168]{1,0:T(8,128)(2,1)S(1)}, u32[]{:S(2)}, u32[]{:S(2)}) collective-permute-start(bf16[128,7168]{1,0:T(8,128)(2,1)S(1)} %collective-permute-done.10), channel_id=1, source_target_pairs={{0,2},{2,4},{4,6},{6,8},{8,10},{10,12},{12,14},{14,16},{16,18},{18... | collective-permute-start | bytes 5505032 | tf_op jit(solution)/shard_map/ppermute | solution.py:24
  328.8 1.3 copy-start.22
  330.1 25.3 %collective-permute-start.12 = (bf16[128,7168]{1,0:T(8,128)(2,1)S(1)}, bf16[128,7168]{1,0:T(8,128)(2,1)S(1)}, u32[]{:S(2)}, u32[]{:S(2)}) collective-permute-start(bf16[128,7168]{1,0:T(8,128)(2,1)S(1)} %collective-permute-done.11), channel_id=1, source_target_pairs={{0,2},{2,4},{4,6},{6,8},{8,10},{10,12},{12,14},{14,16},{16,18},{18... | collective-permute-start | bytes 5505032 | tf_op jit(solution)/shard_map/ppermute | solution.py:24
  356.7 25.5 %collective-permute-start.13 = (bf16[128,7168]{1,0:T(8,128)(2,1)S(1)}, bf16[128,7168]{1,0:T(8,128)(2,1)}, u32[]{:S(2)}, u32[]{:S(2)}) collective-permute-start(bf16[128,7168]{1,0:T(8,128)(2,1)S(1)} %collective-permute-done.12), channel_id=1, source_target_pairs={{0,2},{2,4},{4,6},{6,8},{8,10},{10,12},{12,14},{14,16},{16,18},{18... | collective-permute-start | bytes 5505032 | tf_op jit(solution)/shard_map/ppermute | solution.py:24
  382.1 25.7 %collective-permute-start.14 = (bf16[128,7168]{1,0:T(8,128)(2,1)}, bf16[128,7168]{1,0:T(8,128)(2,1)}, u32[]{:S(2)}, u32[]{:S(2)}) collective-permute-start(bf16[128,7168]{1,0:T(8,128)(2,1)} %collective-permute-done.13), channel_id=1, source_target_pairs={{0,2},{2,4},{4,6},{6,8},{8,10},{10,12},{12,14},{14,16},{16,18},{18... | collective-permute-start | bytes 5505032 | tf_op jit(solution)/shard_map/ppermute | solution.py:24
  382.1 75.8 %copy-start.25 = (bf16[128,7168]{1,0:T(8,128)(2,1)S(1)}, bf16[128,7168]{1,0:T(8,128)(2,1)}, u32[]{:S(2)}) copy-start(bf16[128,7168]{1,0:T(8,128)(2,1)} %copy-done.24) | copy-start | bytes 5505028
  382.1 77.2 %copy-start.23 = (bf16[128,7168]{1,0:T(8,128)(2,1)S(1)}, bf16[128,7168]{1,0:T(8,128)(2,1)}, u32[]{:S(2)}) copy-start(bf16[128,7168]{1,0:T(8,128)(2,1)} %copy-done.22) | copy-start | bytes 5505028
  382.1 78.6 %copy-start.21 = (bf16[128,7168]{1,0:T(8,128)(2,1)S(1)}, bf16[128,7168]{1,0:T(8,128)(2,1)}, u32[]{:S(2)}) copy-start(bf16[128,7168]{1,0:T(8,128)(2,1)} %copy-done.20) | copy-start | bytes 5505028
  382.1 80.0 %copy-start.19 = (bf16[128,7168]{1,0:T(8,128)(2,1)S(1)}, bf16[128,7168]{1,0:T(8,128)(2,1)}, u32[]{:S(2)}) copy-start(bf16[128,7168]{1,0:T(8,128)(2,1)} %copy-done.18) | copy-start | bytes 5505028
  382.1 81.3 %copy-start.17 = (bf16[128,7168]{1,0:T(8,128)(2,1)S(1)}, bf16[128,7168]{1,0:T(8,128)(2,1)}, u32[]{:S(2)}) copy-start(bf16[128,7168]{1,0:T(8,128)(2,1)} %copy-done.16) | copy-start | bytes 5505028
  382.1 82.7 %copy-start.15 = (bf16[128,7168]{1,0:T(8,128)(2,1)S(1)}, bf16[128,7168]{1,0:T(8,128)(2,1)}, u32[]{:S(2)}) copy-start(bf16[128,7168]{1,0:T(8,128)(2,1)} %copy-done.14) | copy-start | bytes 5505028
  382.1 84.1 %copy-start.13 = (bf16[128,7168]{1,0:T(8,128)(2,1)S(1)}, bf16[128,7168]{1,0:T(8,128)(2,1)}, u32[]{:S(2)}) copy-start(bf16[128,7168]{1,0:T(8,128)(2,1)} %copy-done.12) | copy-start | bytes 5505028
  382.2 85.5 %copy-start.11 = (bf16[128,7168]{1,0:T(8,128)(2,1)S(1)}, bf16[128,7168]{1,0:T(8,128)(2,1)}, u32[]{:S(2)}) copy-start(bf16[128,7168]{1,0:T(8,128)(2,1)} %copy-done.10) | copy-start | bytes 5505028
  382.2 86.9 %copy-start.9 = (bf16[128,7168]{1,0:T(8,128)(2,1)S(1)}, bf16[128,7168]{1,0:T(8,128)(2,1)}, u32[]{:S(2)}) copy-start(bf16[128,7168]{1,0:T(8,128)(2,1)} %copy-done.8) | copy-start | bytes 5505028
  382.2 88.2 %copy-start.7 = (bf16[128,7168]{1,0:T(8,128)(2,1)S(1)}, bf16[128,7168]{1,0:T(8,128)(2,1)}, u32[]{:S(2)}) copy-start(bf16[128,7168]{1,0:T(8,128)(2,1)} %copy-done.6) | copy-start | bytes 5505028
  382.2 89.6 %copy-start.5 = (bf16[128,7168]{1,0:T(8,128)(2,1)S(1)}, bf16[128,7168]{1,0:T(8,128)(2,1)}, u32[]{:S(2)}) copy-start(bf16[128,7168]{1,0:T(8,128)(2,1)} %copy-done.4) | copy-start | bytes 5505028
  382.2 90.9 %copy-start.3 = (bf16[128,7168]{1,0:T(8,128)(2,1)S(1)}, bf16[128,7168]{1,0:T(8,128)(2,1)}, u32[]{:S(2)}) copy-start(bf16[128,7168]{1,0:T(8,128)(2,1)} %copy-done.2) | copy-start | bytes 5505028
  382.2 92.3 %copy-start.1 = (bf16[128,7168]{1,0:T(8,128)(2,1)S(1)}, bf16[128,7168]{1,0:T(8,128)(2,1)}, u32[]{:S(2)}) copy-start(bf16[128,7168]{1,0:T(8,128)(2,1)} %copy-done) | copy-start | bytes 5505028
  (10 other events, 12.5 us)
Sparse Core Ops, SparseCore 0:
  483.7 89.9 all-gather.1
